TPU v7x, 32 devices: a whole 2x2x4 slice. The times are simulated.
32 devices in a mesh: cfg: 2 (over y), space: 8 (over z, x), tm: 2 (over core).
Axes of the slice: x: 2, y: 2, z: 4, core: 2. Of those that a mesh axis runs over, the one named last changes fastest.
Arguments:
- eigvecs: bfloat16 [4, 2304, 3, 2, 128], P(('cfg', 'tm'), 'space'), parts along dimension 0, may hold values from -6 to 6
- perambulator: bfloat16 [4, 8, 4, 2, 128, 128], P(('cfg', 'tm'), None, None, None, 'space'), parts along dimension 0, may hold values from -1 to 4
- momenta: int32 [1, 3], replicated, may hold values from 1 to 3
- source_slots: int32 [2], replicated, may hold values from 0 to 7, as said below
- gamma_columns: int32 [12, 4], replicated, may hold values from 0 to 3, each once within a row
- gamma_phases: int32 [12, 4], replicated, may hold values from 0 to 3
Outputs:
- meson: float32 [4, 128, 1, 12, 2, 128], P(('cfg', 'tm'), 'space'), parts along dimension 0
There are 2 independent parts, one for each index of `cfg`. A program takes and returns all parts, laid end to end along the dimension named above; an argument that names none is the same for every part. Nothing has to cross between parts.
Inputs may be any that keep to these rules, and one draw needn't show every extreme that they name: `source_slots`: the two slots differ, and one of them is 7. `gamma_columns`: each row is a permutation of 0 to 3.
All inputs are finite; a program needn't handle non-finite values.
Results may differ from a plain program's by a relative error of at most 0.0049.
Values may be sent and summed in bfloat16 or wider, within the bound.
A program may use at most 64 MiB of HBM per device.

v0:
```python
import functools
import math

import jax
import jax.numpy as jnp
from jax import lax
from jax.experimental import pallas as pl
from jax.experimental.pallas import tpu as pltpu
from jax.sharding import PartitionSpec as P

LY = 48
LZ = 48
WIRE = jnp.bfloat16
F32 = jnp.float32
BF16 = jnp.bfloat16
MESH = pl.DeviceIdType.MESH


def site_phases(momenta_at, first_site, site_count, extent_x, shape):
    site = (lax.broadcasted_iota(jnp.int32, shape, 0) + first_site).astype(F32)
    lines = jnp.floor((site + 0.5) * (1.0 / LZ))
    coord_x = jnp.floor((lines + 0.5) * (1.0 / LY))
    coord_y = lines - LY * coord_x
    coord_z = site - LZ * lines

    def share(momentum, coord, extent):
        turn = momentum.astype(F32) * coord * (1.0 / extent)
        return turn - jnp.floor(turn)

    turns = (
        share(momenta_at(0), coord_x, extent_x)
        + share(momenta_at(1), coord_y, LY)
        + share(momenta_at(2), coord_z, LZ)
    )
    turns = turns - jnp.floor(turns + 0.5)
    half = math.pi * turns
    square = half * half
    sine = jnp.full(shape, 1.0 / 6227020800.0, F32)
    for term in (-1.0 / 39916800.0, 1.0 / 362880.0, -1.0 / 5040.0, 1.0 / 120.0, -1.0 / 6.0, 1.0):
        sine = sine * square + term
    sine = sine * half
    cosine = jnp.full(shape, 1.0 / 479001600.0, F32)
    for term in (-1.0 / 3628800.0, 1.0 / 40320.0, -1.0 / 720.0, 1.0 / 24.0, -0.5, 1.0):
        cosine = cosine * square + term
    return 1.0 - 2.0 * sine * sine, 2.0 * sine * cosine


def kernel(
    n, sites, extent_x, factor,
    momenta, slots, columns, phases, eig_hbm, per_hbm, out_ref,
    eig, eig32, left, right, per, sink, turned, crossing, picked, wide, part, sums, mfull, mixed, blocks,
    load_sem, own_send, own_recv, fwd_send, fwd_recv,
    turn_send, turn_recv, red_send, red_recv, all_send, all_recv,
):
    me = lax.axis_index("space")
    eig_count = eig.shape[1]
    rows = eig_count // n
    gammas = columns.shape[1]

    load_per = pltpu.make_async_copy(per_hbm, per, load_sem.at[0])
    load_eig = pltpu.make_async_copy(eig_hbm, eig, load_sem.at[1])
    load_per.start()
    load_eig.start()

    hubs = n // 2
    hub_rows = eig_count // hubs
    slot = me - n // 4
    is_hub = (slot >= 0) & (slot < hubs)
    side = lax.rem(me, 2)
    partner = me + 1 - 2 * side
    corner = n - 1 - me

    barrier = pltpu.get_barrier_semaphore()

    def greet(peer):
        pl.semaphore_signal(barrier, inc=1, device_id={"space": peer}, device_id_type=MESH)

    for k in range(1, n):
        peer = lax.rem(me + k, n)
        pl.when(is_hub | (peer != corner))(functools.partial(greet, peer))

    load_per.wait()
    mine = pl.ds(pl.multiple_of(me * rows, rows), rows)
    sink[:, :, mine, :] = per[slots[1]]
    first = per[slots[0]].reshape(8 * rows, eig_count).astype(F32)
    turned[...] = first.T.astype(BF16).reshape(n, rows, 8 * rows)

    def remote(src, dst, send, recv, peer):
        return pltpu.make_async_remote_copy(
            src_ref=src, dst_ref=dst, send_sem=send, recv_sem=recv,
            device_id={"space": peer}, device_id_type=MESH,
        )

    def sink_of(owner):
        return sink.at[:, :, pl.ds(pl.multiple_of(owner * rows, rows), rows), :]

    load_eig.wait()
    eig32[...] = eig[...].astype(F32)
    cosine, sine = site_phases(lambda i: momenta[0, i], me * sites, sites, extent_x, (sites, eig_count))
    for color in range(3):
        real = eig32[pl.ds(2 * color, sites, stride=6), :]
        imag = eig32[pl.ds(2 * color + 1, sites, stride=6), :]
        wave_real = (cosine * real - sine * imag).astype(BF16)
        wave_imag = (sine * real + cosine * imag).astype(BF16)
        low = pl.ds(2 * color * sites, sites)
        high = pl.ds((2 * color + 1) * sites, sites)
        left[low, :] = real.astype(BF16)
        left[high, :] = imag.astype(BF16)
        right[low, :eig_count] = wave_real
        right[low, eig_count:] = wave_imag
        right[high, :eig_count] = wave_imag
        right[high, eig_count:] = -wave_real
    whole = lax.dot_general(
        left[...], right[...], (((0,), (0,)), ((), ())), preferred_element_type=F32
    )
    part[...] = whole.astype(part.dtype).reshape(hubs, hub_rows, 2 * eig_count)

    pl.semaphore_wait(barrier, n - 2 + is_hub.astype(jnp.int32))

    def red(j):
        return remote(part.at[j], sums.at[me], red_send.at[j], red_recv.at[me], j + n // 4)

    for i in range(hubs):
        j = jnp.where(me < n // 2, hubs - 1 - i, i)
        pl.when(slot != j)(functools.partial(lambda j: red(j).start(), j))

    near = remote(sink_of(me), sink_of(me), own_send.at[0], own_recv.at[0], partner)
    near_turn = remote(turned.at[partner], picked.at[me], turn_send.at[0], turn_recv.at[0], partner)
    line = lax.div(me, 2)
    lines = n // 2
    lower = line < lines // 2
    mirror = jnp.where(lower, line, lines - 1 - line)

    def other_line(k):
        far = lines - 1 - k
        far = far - (far <= mirror).astype(jnp.int32)
        return jnp.where(lower, far, lines - 1 - far)

    def cross(k, target, origin):
        peer = 2 * target + side
        pair = pl.ds(pl.multiple_of(2 * target, 2), 2)
        owner = 2 * origin + side
        return (
            remote(
                turned.at[pair], crossing.at[origin], turn_send.at[1 + k],
                turn_recv.at[1 + origin], peer,
            ),
            remote(
                sink_of(owner), sink_of(owner), own_send.at[1 + k], own_recv.at[1 + origin], peer
            ),
        )

    own = []
    for k in range(lines - 1):
        own.extend(cross(k, other_line(k), line))
    for copy in [near_turn] + own + [near]:
        copy.start()

    def gather(k):
        peer = lax.rem(me + k, n)
        here = jnp.clip(slot, 0, hubs - 1)
        return remote(mfull.at[here], mfull.at[here], all_send.at[k], all_recv.at[here], peer)

    @pl.when(is_hub)
    def _():
        total = part[jnp.clip(slot, 0, hubs - 1)].astype(F32)
        for k in range(1, n):
            source = lax.rem(me + k, n)
            remote(part.at[0], sums.at[source], red_send.at[0], red_recv.at[source], source).wait_recv()
            total = total + sums[source].astype(F32)
        mfull[jnp.clip(slot, 0, hubs - 1)] = total.astype(BF16)
        for k in range(1, n):
            gather(k).start()

    fwds = []
    for k in range(lines - 1):
        origin = other_line(lines - 2 - k)
        for copy in cross(0, origin, origin):
            copy.wait_recv()
        owner = 2 * origin + side
        fwds.append(
            remote(
                crossing.at[origin, 1 - side], picked.at[owner],
                fwd_send.at[k + lines], fwd_recv.at[origin + lines], partner,
            )
        )
        fwds.append(
            remote(sink_of(owner), sink_of(owner), fwd_send.at[k], fwd_recv.at[origin], partner)
        )
        fwds[-2].start()
        fwds[-1].start()
        picked[owner] = crossing[origin, side]
    picked[me] = turned[me]
    near_turn.wait_recv()
    near.wait_recv()
    for copy in fwds:
        copy.wait_recv()

    spin_of = lax.broadcasted_iota(jnp.int32, (rows, 8 * rows), 1) // (2 * rows)
    for k in range(n):
        block = picked[k].astype(F32)
        for spin in range(4):
            wide[pl.ds(spin * rows, rows), pl.ds(k * 8 * rows, 8 * rows)] = jnp.where(
                spin_of == spin, block, 0.0
            ).astype(BF16)
    for j in range(hubs):
        arrival = remote(mfull.at[j], mfull.at[j], all_send.at[0], all_recv.at[j], partner)
        pl.when(slot != j)(arrival.wait_recv)
        for half in range(2):
            block = mfull[j, half * rows : (half + 1) * rows]
            turned_block = jnp.concatenate([block[:, eig_count:], -block[:, :eig_count]], axis=1)
            for spin in range(4):
                base = (2 * j + half) * 8 * rows + spin * 2 * rows
                mixed[pl.ds(base, rows), :] = block
                mixed[pl.ds(base + rows, rows), :] = turned_block
    cross = jnp.dot(wide[...], mixed[...], preferred_element_type=F32)
    cross_real, cross_imag = cross[:, :eig_count], cross[:, eig_count:]
    stacked = jnp.concatenate(
        [
            jnp.concatenate([cross_real, -cross_imag], axis=1),
            jnp.concatenate([cross_imag, cross_real], axis=1),
        ],
        axis=0,
    ).astype(BF16)
    for pair in range(2):
        table = jnp.concatenate(
            [sink[2 * pair + i].reshape(2 * eig_count, eig_count) for i in range(2)], axis=1
        )
        result = jnp.dot(stacked, table, preferred_element_type=F32) * factor
        for i in range(2):
            for half in range(2):
                for spin in range(4):
                    base = (half * 4 + spin) * rows
                    blocks[half, spin * 4 + 2 * pair + i] = result[
                        base : base + rows, i * eig_count : (i + 1) * eig_count
                    ]
    for g in range(gammas):
        real = imag = None
        for spin in range(4):
            phase = phases[spin, g]
            odd = phase % 2
            index = spin * 4 + columns[spin, g]
            sign_real = jnp.where((phase == 0) | (phase == 3), 1.0, -1.0).astype(F32)
            sign_imag = jnp.where(phase < 2, 1.0, -1.0).astype(F32)
            term_real = sign_real * blocks[odd, index]
            term_imag = sign_imag * blocks[1 - odd, index]
            real = term_real if real is None else real + term_real
            imag = term_imag if imag is None else imag + term_imag
        out_ref[pl.ds(2 * g, rows, stride=2 * gammas), :] = real
        out_ref[pl.ds(2 * g + 1, rows, stride=2 * gammas), :] = imag

    for copy in own + fwds + [near, near_turn]:
        copy.wait_send()
    for j in range(hubs):
        pl.when(slot != j)(lambda j=j: red(j).wait_send())

    @pl.when(is_hub)
    def _():
        for k in range(1, n):
            gather(k).wait_send()


def on_device_kernel(eigvecs, perambulator, momenta, source_slots, gamma_columns, gamma_phases):
    sites, eig_count = eigvecs.shape[1], eigvecs.shape[4]
    n = lax.axis_size("space")
    rows = eig_count // n
    total_sites = sites * n
    gammas = gamma_columns.shape[0]
    stored = perambulator.shape[1]
    body = functools.partial(
        kernel, n, sites, total_sites // (LY * LZ), 1.0 / math.sqrt(12.0 * total_sites)
    )
    dma = pltpu.SemaphoreType.DMA
    smem = pl.BlockSpec(memory_space=pltpu.SMEM)
    hbm = pl.BlockSpec(memory_space=pl.ANY)
    out = pl.pallas_call(
        body,
        out_shape=jax.ShapeDtypeStruct((rows * gammas * 2, eig_count), F32),
        in_specs=[smem, smem, smem, smem, hbm, hbm],
        out_specs=pl.BlockSpec(memory_space=pltpu.VMEM),
        scratch_shapes=[
            pltpu.VMEM((sites * 6, eig_count), BF16),
            pltpu.VMEM((sites * 6, eig_count), F32),
            pltpu.VMEM((sites * 6, eig_count), BF16),
            pltpu.VMEM((sites * 6, 2 * eig_count), BF16),
            pltpu.VMEM((stored, 4, 2, rows, eig_count), BF16),
            pltpu.VMEM((4, 2, eig_count, eig_count), BF16),
            pltpu.VMEM((n, rows, 8 * rows), BF16),
            pltpu.VMEM((n // 2, 2, rows, 8 * rows), BF16),
            pltpu.VMEM((n, rows, 8 * rows), BF16),
            pltpu.VMEM((4 * rows, 8 * eig_count), BF16),
            pltpu.VMEM((n // 2, 2 * rows, 2 * eig_count), WIRE),
            pltpu.VMEM((n, 2 * rows, 2 * eig_count), WIRE),
            pltpu.VMEM((n // 2, 2 * rows, 2 * eig_count), BF16),
            pltpu.VMEM((8 * eig_count, 2 * eig_count), BF16),
            pltpu.VMEM((2, 16, rows, eig_count), F32),
            dma((2,)),
        ]
        + [dma((n,)) for _ in range(10)],
        compiler_params=pltpu.CompilerParams(collective_id=0, has_side_effects=True),
    )(
        momenta,
        source_slots,
        gamma_columns.T,
        gamma_phases.T,
        eigvecs.reshape(sites * 6, eig_count),
        perambulator[0],
    )
    return out.reshape(1, rows, 1, gammas, 2, eig_count)


def on_device_plain(eigvecs, perambulator, momenta, source_slots, gamma_columns, gamma_phases):
    sites, eig_count = eigvecs.shape[1], eigvecs.shape[4]
    n = lax.axis_size("space")
    total_sites = sites * n
    extent_x = total_sites // (LY * LZ)
    factor = 1.0 / math.sqrt(12.0 * total_sites)
    first_site = lax.axis_index("space") * sites
    chosen = jnp.take(perambulator[0], source_slots, axis=0)
    sinks = lax.all_gather(chosen[1], "space", axis=2, tiled=True)
    turned = lax.all_to_all(chosen[0], "space", split_axis=3, concat_axis=2, tiled=True)
    real = eigvecs[0, :, :, 0].astype(F32)
    imag = eigvecs[0, :, :, 1].astype(F32)
    flat = eigvecs[0].reshape(sites * 6, eig_count)
    tables = []
    for p in range(momenta.shape[0]):
        cosine, sine = site_phases(
            lambda i, p=p: momenta[p, i], first_site, sites, extent_x, (sites, 1, 1)
        )
        wave_real = cosine * real - sine * imag
        wave_imag = sine * real + cosine * imag
        upper = jnp.concatenate([wave_real, wave_imag], axis=2)
        lower = jnp.concatenate([wave_imag, -wave_real], axis=2)
        waves = jnp.stack([upper, lower], axis=2).astype(BF16).reshape(sites * 6, 2 * eig_count)
        tables.append(
            lax.dot_general(flat, waves, (((0,), (0,)), ((), ())), preferred_element_type=F32)
        )
    whole = lax.psum(jnp.stack(tables), "space").astype(BF16)
    turned_whole = jnp.concatenate([whole[:, :, eig_count:], -whole[:, :, :eig_count]], axis=2)
    both = jnp.stack([whole, turned_whole], axis=1)
    cross = jnp.einsum("skla,pklm->aspm", turned, both, preferred_element_type=F32)
    cross_real, cross_imag = cross[..., :eig_count], cross[..., eig_count:]
    stacked = jnp.stack(
        [
            jnp.stack([cross_real, -cross_imag], axis=-2),
            jnp.stack([cross_imag, cross_real], axis=-2),
        ],
        axis=3,
    ).astype(BF16)
    blocks = jnp.einsum("asphkl,tklb->apsthb", stacked, sinks, preferred_element_type=F32)
    spins = jnp.arange(4, dtype=jnp.int32)
    matches = (gamma_columns[:, :, None] == spins).astype(F32)
    real_sign = (gamma_phases == 0).astype(F32) - (gamma_phases == 2).astype(F32)
    imag_sign = (gamma_phases == 1).astype(F32) - (gamma_phases == 3).astype(F32)
    mix_real = matches * real_sign[:, :, None]
    mix_imag = matches * imag_sign[:, :, None]
    mix = jnp.stack(
        [jnp.stack([mix_real, -mix_imag], axis=-1), jnp.stack([mix_imag, mix_real], axis=-1)],
        axis=1,
    )
    meson = factor * jnp.einsum("gosth,apsthb->apgob", mix, blocks, precision=lax.Precision.HIGHEST)
    return meson[None]


def on_device(eigvecs, perambulator, momenta, *rest):
    n = lax.axis_size("space")
    rows = perambulator.shape[4]
    small = eigvecs.shape[1] % 16 == 0 and eigvecs.shape[4] == 128
    if rows % 16 == 0 and n % 4 == 0 and momenta.shape[0] == 1 and small:
        return on_device_kernel(eigvecs, perambulator, momenta, *rest)
    return on_device_plain(eigvecs, perambulator, momenta, *rest)


def solution(mesh):
    in_specs = (
        P(("cfg", "tm"), "space", None, None, None),
        P(("cfg", "tm"), None, None, None, "space", None),
        P(),
        P(),
        P(),
        P(),
    )
    out_specs = P(("cfg", "tm"), "space", None, None, None, None)
    return jax.shard_map(
        on_device, mesh=mesh, in_specs=in_specs, out_specs=out_specs, check_vma=False
    )
```

profile of v0, /device:TPU:0, one launch (start us, length us, event | category | flops | bytes accessed | tf_op | source)
XLA Modules:
  0.0 19.9 jit_solution(3093985983020658104)
XLA Ops:
  0.0 18.3 %shard_map.64 = f32[384,128]{1,0:T(8,128)} custom-call(s32[1,3]{1,0:T(1,128)} %momenta.1, s32[2]{0:T(128)} %slots.1, s32[4,12]{1,0:T(4,128)} %bitcast.10, s32[4,12]{1,0:T(4,128)} %bitcast.11, bf16[1728,128]{1,0:T(8,128)(2,1)} %bitcast.8, bf16[8,4,2,16,128]{4,3,2,1,0:T(8,128)(2,1)} %bitcast.9), custom_call_target="tpu_custom_call" | custom-call | tf_op jit(solution)/shard_map/pallas_call | solution.py:276
  18.3 1.6 %copy.9 = f32[1,16,1,12,2,128]{5,4,3,2,1,0:T(2,128)} copy(f32[1,16,1,12,2,128]{5,4,3,2,1,0:T(2,128)} %bitcast.7) | data formatting | bytes 393216
where the time goes:
time: 20.1 us; the launch traced here: 19.9 us
  Pallas kernels  18.3 us (91%)
  local copies, waits for them, and re-layouts  1.62 us (8%)
    pallas_call x1, Pallas kernels, on_device_kernel(): pl.pallas_call(body, out_shape=jax.ShapeDtypeStruct((rows * gammas * 2, e...  18.3 us
    unnamed x1, local copies, waits for them, and re-layouts  1.62 us

commit v1 on v0

--- a/solution.py
+++ b/solution.py
@@ -14,6 +14,7 @@
 F32 = jnp.float32
 BF16 = jnp.bfloat16
 MESH = pl.DeviceIdType.MESH
+VMEM_LIMIT = 32 * 1024 * 1024
 
 
 def site_phases(momenta_at, first_site, site_count, extent_x, shape):
@@ -47,8 +48,8 @@
 
 def kernel(
     n, sites, extent_x, factor,
-    momenta, slots, columns, phases, eig_hbm, per_hbm, out_ref,
-    eig, eig32, left, right, per, sink, turned, crossing, picked, wide, part, sums, mfull, mixed, blocks,
+    momenta_hbm, slots_hbm, columns_hbm, phases_hbm, eig_hbm, per_hbm, out_ref,
+    momenta, slots, columns, phases, eig, eig32, left, right, per, sink, turned, crossing, picked, wide, part, sums, mfull, mixed, blocks,
     load_sem, own_send, own_recv, fwd_send, fwd_recv,
     turn_send, turn_recv, red_send, red_recv, all_send, all_recv,
 ):
@@ -59,8 +60,12 @@
 
     load_per = pltpu.make_async_copy(per_hbm, per, load_sem.at[0])
     load_eig = pltpu.make_async_copy(eig_hbm, eig, load_sem.at[1])
-    load_per.start()
-    load_eig.start()
+    load_slots = pltpu.make_async_copy(slots_hbm, slots, load_sem.at[2])
+    load_momenta = pltpu.make_async_copy(momenta_hbm, momenta, load_sem.at[3])
+    load_columns = pltpu.make_async_copy(columns_hbm, columns, load_sem.at[4])
+    load_phases = pltpu.make_async_copy(phases_hbm, phases, load_sem.at[5])
+    for load in (load_eig, load_momenta, load_slots, load_per, load_columns, load_phases):
+        load.start()
 
     hubs = n // 2
     hub_rows = eig_count // hubs
@@ -79,6 +84,7 @@
         peer = lax.rem(me + k, n)
         pl.when(is_hub | (peer != corner))(functools.partial(greet, peer))
 
+    load_slots.wait()
     load_per.wait()
     mine = pl.ds(pl.multiple_of(me * rows, rows), rows)
     sink[:, :, mine, :] = per[slots[1]]
@@ -94,6 +100,7 @@
     def sink_of(owner):
         return sink.at[:, :, pl.ds(pl.multiple_of(owner * rows, rows), rows), :]
 
+    load_momenta.wait()
     load_eig.wait()
     eig32[...] = eig[...].astype(F32)
     cosine, sine = site_phases(lambda i: momenta[0, i], me * sites, sites, extent_x, (sites, eig_count))
@@ -196,6 +203,8 @@
     for copy in fwds:
         copy.wait_recv()
 
+    load_columns.wait()
+    load_phases.wait()
     spin_of = lax.broadcasted_iota(jnp.int32, (rows, 8 * rows), 1) // (2 * rows)
     for k in range(n):
         block = picked[k].astype(F32)
@@ -260,6 +269,12 @@
             gather(k).wait_send()
 
 
+def store_kernel(source, target, sem):
+    copy = pltpu.make_async_copy(source, target, sem.at[0])
+    copy.start()
+    copy.wait()
+
+
 def on_device_kernel(eigvecs, perambulator, momenta, source_slots, gamma_columns, gamma_phases):
     sites, eig_count = eigvecs.shape[1], eigvecs.shape[4]
     n = lax.axis_size("space")
@@ -271,14 +286,17 @@
         kernel, n, sites, total_sites // (LY * LZ), 1.0 / math.sqrt(12.0 * total_sites)
     )
     dma = pltpu.SemaphoreType.DMA
-    smem = pl.BlockSpec(memory_space=pltpu.SMEM)
-    hbm = pl.BlockSpec(memory_space=pl.ANY)
+    hbm = pl.BlockSpec(memory_space=pltpu.HBM)
     out = pl.pallas_call(
         body,
-        out_shape=jax.ShapeDtypeStruct((rows * gammas * 2, eig_count), F32),
-        in_specs=[smem, smem, smem, smem, hbm, hbm],
+        out_shape=pltpu.VMEM((rows * gammas * 2, eig_count), F32),
+        in_specs=[hbm] * 6,
         out_specs=pl.BlockSpec(memory_space=pltpu.VMEM),
         scratch_shapes=[
+            pltpu.SMEM(momenta.shape, jnp.int32),
+            pltpu.SMEM(source_slots.shape, jnp.int32),
+            pltpu.SMEM((4, gammas), jnp.int32),
+            pltpu.SMEM((4, gammas), jnp.int32),
             pltpu.VMEM((sites * 6, eig_count), BF16),
             pltpu.VMEM((sites * 6, eig_count), F32),
             pltpu.VMEM((sites * 6, eig_count), BF16),
@@ -294,19 +312,34 @@
             pltpu.VMEM((n // 2, 2 * rows, 2 * eig_count), BF16),
             pltpu.VMEM((8 * eig_count, 2 * eig_count), BF16),
             pltpu.VMEM((2, 16, rows, eig_count), F32),
-            dma((2,)),
+            dma((6,)),
         ]
         + [dma((n,)) for _ in range(10)],
-        compiler_params=pltpu.CompilerParams(collective_id=0, has_side_effects=True),
+        compiler_params=pltpu.CompilerParams(
+            collective_id=0, has_side_effects=True, vmem_limit_bytes=VMEM_LIMIT
+        ),
     )(
-        momenta,
-        source_slots,
-        gamma_columns.T,
-        gamma_phases.T,
-        eigvecs.reshape(sites * 6, eig_count),
-        perambulator[0],
-    )
-    return out.reshape(1, rows, 1, gammas, 2, eig_count)
+        *(
+            pltpu.with_memory_space_constraint(array, pltpu.HBM)
+            for array in (
+                momenta,
+                source_slots,
+                gamma_columns.T,
+                gamma_phases.T,
+                eigvecs.reshape(sites * 6, eig_count),
+                perambulator[0],
+            )
+        )
+    )
+    done = pl.pallas_call(
+        store_kernel,
+        out_shape=jax.ShapeDtypeStruct(out.shape, F32),
+        in_specs=[pl.BlockSpec(memory_space=pl.ANY)],
+        out_specs=hbm,
+        scratch_shapes=[dma((1,))],
+        compiler_params=pltpu.CompilerParams(vmem_limit_bytes=VMEM_LIMIT),
+    )(out)
+    return done.reshape(1, rows, 1, gammas, 2, eig_count)
 
 
 def on_device_plain(eigvecs, perambulator, momenta, source_slots, gamma_columns, gamma_phases):

time: 20.1 us -> 17.8 us (0.89)
  local copies, waits for them, and re-layouts: 1.62 us -> 0 us
  Pallas kernels: 18.3 us -> 17.7 us
    unnamed x1 -> x0, local copies, waits for them, and re-layouts: 1.62 us -> none
    pallas_call x1 -> x2, Pallas kernels: 18.3 us -> 17.7 us  [the longest x1 17 us: on_device_kernel(): pl.pallas_call(body, out_shape=pltpu.VMEM((rows * gammas * 2, eig_count),...]
where the time goes in v1:
time: 17.8 us; the launch traced here: 17.7 us
  Pallas kernels  17.7 us (99%)
    pallas_call x1, Pallas kernels, on_device_kernel(): pl.pallas_call(body, out_shape=pltpu.VMEM((rows * gammas * 2, eig_count),...  17 us
    pallas_call x1, Pallas kernels, on_device_kernel(): pl.pallas_call(store_kernel, out_shape=jax.ShapeDtypeStruct(out.shape, F3...  0.69 us

profile of v1, /device:TPU:0, one launch (start us, length us, event | category | flops | bytes accessed | tf_op | source)
XLA Modules:
  0.0 17.7 jit_solution(5714450458335907983)
XLA Ops:
  0.0 17.0 %shard_map.64.source = f32[384,128]{1,0:T(8,128)S(1)} custom-call(s32[1,3]{1,0:T(1,128)} %momenta_hbm.1, s32[2]{0:T(128)} %slots_hbm.1, s32[4,12]{1,0:T(4,128)} %bitcast.9, s32[4,12]{1,0:T(4,128)} %bitcast.10, bf16[1728,128]{1,0:T(8,128)(2,1)} %bitcast.7, bf16[8,4,2,16,128]{4,3,2,1,0:T(8,128)(2,1)} %bitcast.8), custom_call_target="tpu_custom_call" | custom-call | tf_op jit(solution)/shard_map/pallas_call | solution.py:290
  17.0 0.7 %shard_map.65 = f32[384,128]{1,0:T(8,128)} custom-call(f32[384,128]{1,0:T(8,128)S(1)} %shard_map.64.source), custom_call_target="tpu_custom_call" | custom-call | tf_op jit(solution)/shard_map/pallas_call | solution.py:334

commit v2 on v1

--- a/solution.py
+++ b/solution.py
@@ -49,14 +49,23 @@
 def kernel(
     n, sites, extent_x, factor,
     momenta_hbm, slots_hbm, columns_hbm, phases_hbm, eig_hbm, per_hbm, out_ref,
-    momenta, slots, columns, phases, eig, eig32, left, right, per, sink, turned, crossing, picked, wide, part, sums, mfull, mixed, blocks,
-    load_sem, own_send, own_recv, fwd_send, fwd_recv,
-    turn_send, turn_recv, red_send, red_recv, all_send, all_recv,
+    momenta, slots, columns, phases, eig, eig32, waves, left, right, per, sink, turned, picked,
+    part, sums, mfull, blocks, volume,
+    load_sem, send_sem, red_recv, all_recv, turn_recv, near_recv, line_recv,
 ):
     me = lax.axis_index("space")
     eig_count = eig.shape[1]
     rows = eig_count // n
     gammas = columns.shape[1]
+    hubs = n // 2
+    hub_rows = eig_count // hubs
+    slot = me - n // 4
+    is_hub = (slot >= 0) & (slot < hubs)
+    here = jnp.clip(slot, 0, hubs - 1)
+    side = lax.rem(me, 2)
+    line = lax.div(me, 2)
+    lines = n // 2
+    partner = me + 1 - 2 * side
 
     load_per = pltpu.make_async_copy(per_hbm, per, load_sem.at[0])
     load_eig = pltpu.make_async_copy(eig_hbm, eig, load_sem.at[1])
@@ -64,25 +73,38 @@
     load_momenta = pltpu.make_async_copy(momenta_hbm, momenta, load_sem.at[3])
     load_columns = pltpu.make_async_copy(columns_hbm, columns, load_sem.at[4])
     load_phases = pltpu.make_async_copy(phases_hbm, phases, load_sem.at[5])
-    for load in (load_eig, load_momenta, load_slots, load_per, load_columns, load_phases):
+    for load in (load_slots, load_momenta, load_per, load_eig, load_columns, load_phases):
         load.start()
 
-    hubs = n // 2
-    hub_rows = eig_count // hubs
-    slot = me - n // 4
-    is_hub = (slot >= 0) & (slot < hubs)
-    side = lax.rem(me, 2)
-    partner = me + 1 - 2 * side
-    corner = n - 1 - me
-
     barrier = pltpu.get_barrier_semaphore()
-
-    def greet(peer):
-        pl.semaphore_signal(barrier, inc=1, device_id={"space": peer}, device_id_type=MESH)
-
     for k in range(1, n):
-        peer = lax.rem(me + k, n)
-        pl.when(is_hub | (peer != corner))(functools.partial(greet, peer))
+        pl.semaphore_signal(
+            barrier, inc=1, device_id={"space": lax.rem(me + k, n)}, device_id_type=MESH
+        )
+
+    def remote(src, dst, recv, peer):
+        return pltpu.make_async_remote_copy(
+            src_ref=src, dst_ref=dst, send_sem=send_sem.at[0], recv_sem=recv,
+            device_id={"space": peer}, device_id_type=MESH,
+        )
+
+    def arrived(ref, sem):
+        pltpu.make_async_copy(ref, ref, sem).wait()
+
+    def sink_of(owner):
+        return sink.at[:, :, pl.ds(pl.multiple_of(owner * rows, rows), rows), :]
+
+    def other_line(k):
+        lower = line < lines // 2
+        mirror = jnp.where(lower, line, lines - 1 - line)
+        near = k + (k >= mirror).astype(jnp.int32)
+        return jnp.where(lower, near, lines - 1 - near)
+
+    def send_sink(target):
+        remote(sink_of(me), sink_of(me), line_recv.at[line], 2 * target + side).start()
+
+    def send_near():
+        remote(sink_of(me), sink_of(me), near_recv.at[0], partner).start()
 
     load_slots.wait()
     load_per.wait()
@@ -90,25 +112,20 @@
     sink[:, :, mine, :] = per[slots[1]]
     first = per[slots[0]].reshape(8 * rows, eig_count).astype(F32)
     turned[...] = first.T.astype(BF16).reshape(n, rows, 8 * rows)
-
-    def remote(src, dst, send, recv, peer):
-        return pltpu.make_async_remote_copy(
-            src_ref=src, dst_ref=dst, send_sem=send, recv_sem=recv,
-            device_id={"space": peer}, device_id_type=MESH,
-        )
-
-    def sink_of(owner):
-        return sink.at[:, :, pl.ds(pl.multiple_of(owner * rows, rows), rows), :]
+    picked[me] = turned[me]
 
     load_momenta.wait()
+    cosine, sine = site_phases(lambda i: momenta[0, i], me * sites, sites, extent_x, (sites, eig_count))
+    waves[0] = cosine
+    waves[1] = sine
+
     load_eig.wait()
     eig32[...] = eig[...].astype(F32)
-    cosine, sine = site_phases(lambda i: momenta[0, i], me * sites, sites, extent_x, (sites, eig_count))
     for color in range(3):
         real = eig32[pl.ds(2 * color, sites, stride=6), :]
         imag = eig32[pl.ds(2 * color + 1, sites, stride=6), :]
-        wave_real = (cosine * real - sine * imag).astype(BF16)
-        wave_imag = (sine * real + cosine * imag).astype(BF16)
+        wave_real = (waves[0] * real - waves[1] * imag).astype(BF16)
+        wave_imag = (waves[1] * real + waves[0] * imag).astype(BF16)
         low = pl.ds(2 * color * sites, sites)
         high = pl.ds((2 * color + 1) * sites, sites)
         left[low, :] = real.astype(BF16)
@@ -122,125 +139,85 @@
     )
     part[...] = whole.astype(part.dtype).reshape(hubs, hub_rows, 2 * eig_count)
 
-    pl.semaphore_wait(barrier, n - 2 + is_hub.astype(jnp.int32))
-
-    def red(j):
-        return remote(part.at[j], sums.at[me], red_send.at[j], red_recv.at[me], j + n // 4)
-
-    for i in range(hubs):
-        j = jnp.where(me < n // 2, hubs - 1 - i, i)
-        pl.when(slot != j)(functools.partial(lambda j: red(j).start(), j))
-
-    near = remote(sink_of(me), sink_of(me), own_send.at[0], own_recv.at[0], partner)
-    near_turn = remote(turned.at[partner], picked.at[me], turn_send.at[0], turn_recv.at[0], partner)
-    line = lax.div(me, 2)
-    lines = n // 2
-    lower = line < lines // 2
-    mirror = jnp.where(lower, line, lines - 1 - line)
-
-    def other_line(k):
-        far = lines - 1 - k
-        far = far - (far <= mirror).astype(jnp.int32)
-        return jnp.where(lower, far, lines - 1 - far)
-
-    def cross(k, target, origin):
-        peer = 2 * target + side
-        pair = pl.ds(pl.multiple_of(2 * target, 2), 2)
-        owner = 2 * origin + side
-        return (
-            remote(
-                turned.at[pair], crossing.at[origin], turn_send.at[1 + k],
-                turn_recv.at[1 + origin], peer,
-            ),
-            remote(
-                sink_of(owner), sink_of(owner), own_send.at[1 + k], own_recv.at[1 + origin], peer
-            ),
-        )
-
-    own = []
-    for k in range(lines - 1):
-        own.extend(cross(k, other_line(k), line))
-    for copy in [near_turn] + own + [near]:
-        copy.start()
-
-    def gather(k):
-        peer = lax.rem(me + k, n)
-        here = jnp.clip(slot, 0, hubs - 1)
-        return remote(mfull.at[here], mfull.at[here], all_send.at[k], all_recv.at[here], peer)
+    def send_red():
+        for i in range(hubs):
+            j = jnp.where(me < n // 2, hubs - 1 - i, i)
+            pl.when(slot != j)(
+                lambda j=j: remote(part.at[j], sums.at[me], red_recv.at[0], j + n // 4).start()
+            )
+
+    def send_turned():
+        for k in range(1, n):
+            peer = lax.rem(me + k, n)
+            remote(turned.at[peer], picked.at[me], turn_recv.at[0], peer).start()
+
+    pl.semaphore_wait(barrier, n - 1)
+    send_red()
+    send_near()
+    for k in reversed(range(lines - 1)):
+        send_sink(other_line(k))
+    send_turned()
 
     @pl.when(is_hub)
     def _():
-        total = part[jnp.clip(slot, 0, hubs - 1)].astype(F32)
+        arrived(sums.at[pl.ds(0, n - 1)], red_recv.at[0])
+        total = part[here].astype(F32)
         for k in range(1, n):
-            source = lax.rem(me + k, n)
-            remote(part.at[0], sums.at[source], red_send.at[0], red_recv.at[source], source).wait_recv()
-            total = total + sums[source].astype(F32)
-        mfull[jnp.clip(slot, 0, hubs - 1)] = total.astype(BF16)
+            total = total + sums[lax.rem(me + k, n)].astype(F32)
+        mfull[here] = total.astype(BF16)
         for k in range(1, n):
-            gather(k).start()
-
-    fwds = []
+            peer = k - 1 + (k - 1 >= me).astype(jnp.int32)
+            remote(mfull.at[here], mfull.at[here], all_recv.at[0], peer).start()
+
     for k in range(lines - 1):
-        origin = other_line(lines - 2 - k)
-        for copy in cross(0, origin, origin):
-            copy.wait_recv()
+        origin = other_line(k)
         owner = 2 * origin + side
-        fwds.append(
-            remote(
-                crossing.at[origin, 1 - side], picked.at[owner],
-                fwd_send.at[k + lines], fwd_recv.at[origin + lines], partner,
-            )
-        )
-        fwds.append(
-            remote(sink_of(owner), sink_of(owner), fwd_send.at[k], fwd_recv.at[origin], partner)
-        )
-        fwds[-2].start()
-        fwds[-1].start()
-        picked[owner] = crossing[origin, side]
-    picked[me] = turned[me]
-    near_turn.wait_recv()
-    near.wait_recv()
-    for copy in fwds:
-        copy.wait_recv()
-
+        arrived(sink_of(owner), line_recv.at[origin])
+        remote(sink_of(owner), sink_of(owner), near_recv.at[0], partner).start()
+
+    arrived(picked.at[pl.ds(0, n - 1)], turn_recv.at[0])
+    group = lax.broadcasted_iota(jnp.int32, (rows, eig_count), 1) // rows
+    chunks = [None] * 8
+    for k in range(n):
+        block = picked[k].astype(F32)
+        for c in range(8):
+            turn = (k - c) % 8
+            moved = pltpu.roll(block, turn * rows, 1) if turn else block
+            chunks[c] = moved if chunks[c] is None else jnp.where(group == k, moved, chunks[c])
+    sources = jnp.concatenate(chunks[0::2] + chunks[1::2], axis=0).astype(BF16)
     load_columns.wait()
     load_phases.wait()
-    spin_of = lax.broadcasted_iota(jnp.int32, (rows, 8 * rows), 1) // (2 * rows)
-    for k in range(n):
-        block = picked[k].astype(F32)
-        for spin in range(4):
-            wide[pl.ds(spin * rows, rows), pl.ds(k * 8 * rows, 8 * rows)] = jnp.where(
-                spin_of == spin, block, 0.0
-            ).astype(BF16)
-    for j in range(hubs):
-        arrival = remote(mfull.at[j], mfull.at[j], all_send.at[0], all_recv.at[j], partner)
-        pl.when(slot != j)(arrival.wait_recv)
-        for half in range(2):
-            block = mfull[j, half * rows : (half + 1) * rows]
-            turned_block = jnp.concatenate([block[:, eig_count:], -block[:, :eig_count]], axis=1)
-            for spin in range(4):
-                base = (2 * j + half) * 8 * rows + spin * 2 * rows
-                mixed[pl.ds(base, rows), :] = block
-                mixed[pl.ds(base + rows, rows), :] = turned_block
-    cross = jnp.dot(wide[...], mixed[...], preferred_element_type=F32)
-    cross_real, cross_imag = cross[:, :eig_count], cross[:, eig_count:]
+    arrived(sink.at[:, :, pl.ds(0, lines * rows), :], near_recv.at[0])
+
+    @pl.when(is_hub)
+    def _():
+        arrived(mfull.at[pl.ds(0, hubs - 1)], all_recv.at[0])
+
+    @pl.when(jnp.logical_not(is_hub))
+    def _():
+        arrived(mfull, all_recv.at[0])
+
+    half = 4 * rows
+    both = jnp.dot(sources, mfull[...].reshape(eig_count, 2 * eig_count), preferred_element_type=F32)
+    cross_real = ((both[:half, :eig_count] + both[half:, eig_count:]) * factor).astype(BF16)
+    cross_imag = ((both[:half, eig_count:] - both[half:, :eig_count]) * factor).astype(BF16)
     stacked = jnp.concatenate(
         [
             jnp.concatenate([cross_real, -cross_imag], axis=1),
             jnp.concatenate([cross_imag, cross_real], axis=1),
         ],
         axis=0,
-    ).astype(BF16)
+    )
     for pair in range(2):
         table = jnp.concatenate(
             [sink[2 * pair + i].reshape(2 * eig_count, eig_count) for i in range(2)], axis=1
         )
-        result = jnp.dot(stacked, table, preferred_element_type=F32) * factor
+        result = jnp.dot(stacked, table, preferred_element_type=F32)
         for i in range(2):
-            for half in range(2):
+            for part_of in range(2):
                 for spin in range(4):
-                    base = (half * 4 + spin) * rows
-                    blocks[half, spin * 4 + 2 * pair + i] = result[
+                    base = (part_of * 4 + spin) * rows
+                    blocks[part_of, spin * 4 + 2 * pair + i] = result[
                         base : base + rows, i * eig_count : (i + 1) * eig_count
                     ]
     for g in range(gammas):
@@ -258,15 +235,17 @@
         out_ref[pl.ds(2 * g, rows, stride=2 * gammas), :] = real
         out_ref[pl.ds(2 * g + 1, rows, stride=2 * gammas), :] = imag
 
-    for copy in own + fwds + [near, near_turn]:
-        copy.wait_send()
-    for j in range(hubs):
-        pl.when(slot != j)(lambda j=j: red(j).wait_send())
+    unit = 4 * rows
+    plain = hubs * unit + 2 * lines * 8 * rows + (n - 1) * rows - 8 * rows
+    extra = (hubs - 1 + n - 1 - hubs) * unit
 
     @pl.when(is_hub)
     def _():
-        for k in range(1, n):
-            gather(k).wait_send()
+        arrived(volume.at[pl.ds(0, plain + extra)], send_sem.at[0])
+
+    @pl.when(jnp.logical_not(is_hub))
+    def _():
+        arrived(volume.at[pl.ds(0, plain)], send_sem.at[0])
 
 
 def store_kernel(source, target, sem):
@@ -299,22 +278,26 @@
             pltpu.SMEM((4, gammas), jnp.int32),
             pltpu.VMEM((sites * 6, eig_count), BF16),
             pltpu.VMEM((sites * 6, eig_count), F32),
+            pltpu.VMEM((2, sites, eig_count), F32),
             pltpu.VMEM((sites * 6, eig_count), BF16),
             pltpu.VMEM((sites * 6, 2 * eig_count), BF16),
             pltpu.VMEM((stored, 4, 2, rows, eig_count), BF16),
             pltpu.VMEM((4, 2, eig_count, eig_count), BF16),
             pltpu.VMEM((n, rows, 8 * rows), BF16),
-            pltpu.VMEM((n // 2, 2, rows, 8 * rows), BF16),
             pltpu.VMEM((n, rows, 8 * rows), BF16),
-            pltpu.VMEM((4 * rows, 8 * eig_count), BF16),
             pltpu.VMEM((n // 2, 2 * rows, 2 * eig_count), WIRE),
             pltpu.VMEM((n, 2 * rows, 2 * eig_count), WIRE),
             pltpu.VMEM((n // 2, 2 * rows, 2 * eig_count), BF16),
-            pltpu.VMEM((8 * eig_count, 2 * eig_count), BF16),
             pltpu.VMEM((2, 16, rows, eig_count), F32),
+            pltpu.VMEM((16 * eig_count, eig_count), BF16),
             dma((6,)),
-        ]
-        + [dma((n,)) for _ in range(10)],
+            dma((1,)),
+            dma((1,)),
+            dma((1,)),
+            dma((1,)),
+            dma((1,)),
+            dma((n // 2,)),
+        ],
         compiler_params=pltpu.CompilerParams(
             collective_id=0, has_side_effects=True, vmem_limit_bytes=VMEM_LIMIT
         ),
@@ -399,7 +382,7 @@
     n = lax.axis_size("space")
     rows = perambulator.shape[4]
     small = eigvecs.shape[1] % 16 == 0 and eigvecs.shape[4] == 128
-    if rows % 16 == 0 and n % 4 == 0 and momenta.shape[0] == 1 and small:
+    if rows == 16 and n == 8 and momenta.shape[0] == 1 and small:
         return on_device_kernel(eigvecs, perambulator, momenta, *rest)
     return on_device_plain(eigvecs, perambulator, momenta, *rest)
 

time: 17.8 us -> 15.8 us (0.89)
  Pallas kernels: 17.7 us -> 15.6 us
    pallas_call x1, Pallas kernels: 17 us -> 14.9 us  [on_device_kernel(): pl.pallas_call(body, out_shape=pltpu.VMEM((rows * gammas * 2, eig_count),...]
where the time goes in v2:
time: 15.8 us; the launch traced here: 15.6 us
  Pallas kernels  15.6 us (99%)
    pallas_call x1, Pallas kernels, on_device_kernel(): pl.pallas_call(body, out_shape=pltpu.VMEM((rows * gammas * 2, eig_count),...  14.9 us
    pallas_call x1, Pallas kernels, on_device_kernel(): pl.pallas_call(store_kernel, out_shape=jax.ShapeDtypeStruct(out.shape, F3...  0.69 us

profile of v2, /device:TPU:0, one launch (start us, length us, event | category | flops | bytes accessed | tf_op | source)
XLA Modules:
  0.0 15.6 jit_solution(1144036108963637377)
XLA Ops:
  0.0 14.9 %shard_map.64.source = f32[384,128]{1,0:T(8,128)S(1)} custom-call(s32[1,3]{1,0:T(1,128)} %momenta_hbm.1, s32[2]{0:T(128)} %slots_hbm.1, s32[4,12]{1,0:T(4,128)} %bitcast.9, s32[4,12]{1,0:T(4,128)} %bitcast.10, bf16[1728,128]{1,0:T(8,128)(2,1)} %bitcast.7, bf16[8,4,2,16,128]{4,3,2,1,0:T(8,128)(2,1)} %bitcast.8), custom_call_target="tpu_custom_call" | custom-call | tf_op jit(solution)/shard_map/pallas_call | solution.py:269
  15.0 0.7 %shard_map.65 = f32[384,128]{1,0:T(8,128)} custom-call(f32[384,128]{1,0:T(8,128)S(1)} %shard_map.64.source), custom_call_target="tpu_custom_call" | custom-call | tf_op jit(solution)/shard_map/pallas_call | solution.py:317

commit v3 on v2

--- a/solution.py
+++ b/solution.py
@@ -50,17 +50,22 @@
     n, sites, extent_x, factor,
     momenta_hbm, slots_hbm, columns_hbm, phases_hbm, eig_hbm, per_hbm, out_ref,
     momenta, slots, columns, phases, eig, eig32, waves, left, right, per, sink, turned, picked,
-    part, sums, mfull, blocks, volume,
-    load_sem, send_sem, red_recv, all_recv, turn_recv, near_recv, line_recv,
+    part, sums, spread, mfull, blocks, volume,
+    ready, reply, load_sem, send_sem, red_recv, all_recv, turn_recv, near_recv, line_recv,
 ):
     me = lax.axis_index("space")
+    time = lax.axis_index("tm")
+    times = lax.axis_size("tm")
+    hub_time = times - 1
     eig_count = eig.shape[1]
     rows = eig_count // n
     gammas = columns.shape[1]
     hubs = n // 2
     hub_rows = eig_count // hubs
     slot = me - n // 4
-    is_hub = (slot >= 0) & (slot < hubs)
+    inner = (slot >= 0) & (slot < hubs)
+    is_hub = inner & (time == hub_time)
+    is_leaf = jnp.logical_not(is_hub)
     here = jnp.clip(slot, 0, hubs - 1)
     side = lax.rem(me, 2)
     line = lax.div(me, 2)
@@ -77,47 +82,85 @@
         load.start()
 
     barrier = pltpu.get_barrier_semaphore()
-    for k in range(1, n):
+
+    def greet(semaphore, peer, peer_time):
         pl.semaphore_signal(
-            barrier, inc=1, device_id={"space": lax.rem(me + k, n)}, device_id_type=MESH
-        )
-
-    def remote(src, dst, recv, peer):
+            semaphore, inc=1, device_id={"space": peer, "tm": peer_time}, device_id_type=MESH
+        )
+
+    def greets(source, source_time, target, target_time):
+        def hub(place, at):
+            return (place >= n // 4) & (place < n // 4 + hubs) & (at == hub_time)
+
+        step = target - source
+        ahead = (step > 0) & (lax.rem(step + n, 2) == 0)
+        pair = (lax.div(source, 2) == lax.div(target, 2)) & (step != 0)
+        near = (source_time == target_time) & (ahead | pair)
+        other = (step != 0) | (source_time != target_time)
+        return other & (hub(source, source_time) | hub(target, target_time) | near)
+
+    expected = 0
+    for other in range(times):
+        for peer in range(n):
+            pl.when(greets(me, time, peer, other))(functools.partial(greet, barrier, peer, other))
+            expected = expected + greets(peer, other, me, time).astype(jnp.int32)
+
+    def remote(src, dst, recv, peer, peer_time=None):
+        peer_time = time if peer_time is None else peer_time
         return pltpu.make_async_remote_copy(
             src_ref=src, dst_ref=dst, send_sem=send_sem.at[0], recv_sem=recv,
-            device_id={"space": peer}, device_id_type=MESH,
+            device_id={"space": peer, "tm": peer_time}, device_id_type=MESH,
         )
 
     def arrived(ref, sem):
         pltpu.make_async_copy(ref, ref, sem).wait()
 
     def sink_of(owner):
-        return sink.at[:, :, pl.ds(pl.multiple_of(owner * rows, rows), rows), :]
-
-    def other_line(k):
-        lower = line < lines // 2
-        mirror = jnp.where(lower, line, lines - 1 - line)
-        near = k + (k >= mirror).astype(jnp.int32)
-        return jnp.where(lower, near, lines - 1 - near)
+        return sink.at[owner]
+
+    late = line >= lines // 2
+    toward = jnp.where(late, 1, -1)
+
+    def enter():
+        pl.semaphore_wait(barrier, expected)
+
+        @pl.when(is_hub)
+        def _():
+            for other in range(times):
+                greet(ready.at[0], me + 2 * toward, other)
+                if other < times - 1:
+                    greet(ready.at[0], me, other)
+
+        for lower in range(lines - 1):
+            pl.when(lower < line)(
+                functools.partial(greet, reply.at[line], 2 * lower + side, time)
+            )
+
+    def send_up(target):
+        pl.semaphore_wait(reply.at[target], 1)
+        send_sink(target)
 
     def send_sink(target):
         remote(sink_of(me), sink_of(me), line_recv.at[line], 2 * target + side).start()
 
     def send_near():
         remote(sink_of(me), sink_of(me), near_recv.at[0], partner).start()
-
-    load_slots.wait()
-    load_per.wait()
-    mine = pl.ds(pl.multiple_of(me * rows, rows), rows)
-    sink[:, :, mine, :] = per[slots[1]]
-    first = per[slots[0]].reshape(8 * rows, eig_count).astype(F32)
-    turned[...] = first.T.astype(BF16).reshape(n, rows, 8 * rows)
-    picked[me] = turned[me]
 
     load_momenta.wait()
     cosine, sine = site_phases(lambda i: momenta[0, i], me * sites, sites, extent_x, (sites, eig_count))
     waves[0] = cosine
     waves[1] = sine
+    load_slots.wait()
+    load_per.wait()
+    sink[me] = per[slots[1]].reshape(8, rows, eig_count)
+
+    early = late & (time == 0)
+
+    @pl.when(early)
+    def _():
+        enter()
+        send_sink(0)
+        send_near()
 
     load_eig.wait()
     eig32[...] = eig[...].astype(F32)
@@ -142,38 +185,72 @@
     def send_red():
         for i in range(hubs):
             j = jnp.where(me < n // 2, hubs - 1 - i, i)
-            pl.when(slot != j)(
-                lambda j=j: remote(part.at[j], sums.at[me], red_recv.at[0], j + n // 4).start()
+            copy = remote(
+                part.at[j], sums.at[time * n + me], red_recv.at[0], j + n // 4, hub_time
             )
+            pl.when((slot != j) | is_leaf)(copy.start)
 
     def send_turned():
         for k in range(1, n):
             peer = lax.rem(me + k, n)
             remote(turned.at[peer], picked.at[me], turn_recv.at[0], peer).start()
 
-    pl.semaphore_wait(barrier, n - 1)
+    pl.when(jnp.logical_not(early))(enter)
     send_red()
-    send_near()
-    for k in reversed(range(lines - 1)):
-        send_sink(other_line(k))
+
+    @pl.when(jnp.logical_not(early))
+    def _():
+        send_near()
+        pl.when(line > 0)(lambda: send_sink(0))
+
+    first = per[slots[0]].reshape(8 * rows, eig_count).astype(F32)
+    turned[...] = first.T.astype(BF16).reshape(n, rows, 8 * rows)
+    picked[me] = turned[me]
+
+    @pl.when(line < lines // 2)
+    def _():
+        pl.when(line == 0)(lambda: send_up(1))
+        send_up(2)
+
+    pl.when(is_leaf)(lambda: pl.semaphore_wait(ready.at[0], 1))
     send_turned()
+    pl.when(line < lines - 1)(lambda: send_up(lines - 1))
+    pl.when(late)(lambda: send_sink(1))
+    pl.when(line == lines - 1)(lambda: send_sink(2))
+
+    def forward(origin):
+        owner = 2 * origin + side
+        arrived(sink.at[owner], line_recv.at[origin])
+        return owner
+
+    def pass_on(origin):
+        owner = forward(origin)
+        remote(sink.at[owner], sink.at[owner], near_recv.at[0], partner).start()
 
     @pl.when(is_hub)
     def _():
-        arrived(sums.at[pl.ds(0, n - 1)], red_recv.at[0])
-        total = part[here].astype(F32)
-        for k in range(1, n):
-            total = total + sums[lax.rem(me + k, n)].astype(F32)
-        mfull[here] = total.astype(BF16)
-        for k in range(1, n):
-            peer = k - 1 + (k - 1 >= me).astype(jnp.int32)
-            remote(mfull.at[here], mfull.at[here], all_recv.at[0], peer).start()
-
-    for k in range(lines - 1):
-        origin = other_line(k)
-        owner = 2 * origin + side
-        arrived(sink_of(owner), line_recv.at[origin])
-        remote(sink_of(owner), sink_of(owner), near_recv.at[0], partner).start()
+        arrived(sums.at[pl.ds(0, times * n - 1)], red_recv.at[0])
+        for other in range(times):
+            own = other == times - 1
+            total = part[here].astype(F32) if own else sums[other * n + me].astype(F32)
+            for k in range(1, n):
+                total = total + sums[other * n + lax.rem(me + k, n)].astype(F32)
+            source = mfull.at[here] if own else spread.at[other]
+            source[...] = total.astype(BF16)
+            for k in range(n - own):
+                peer = k + (k >= me).astype(jnp.int32) if own else k
+                remote(source, mfull.at[here], all_recv.at[0], peer, other).start()
+
+    @pl.when((line > 0) & (line < lines - 1))
+    def _():
+        pass_on(jnp.where(late, 1, 0))
+        pass_on(jnp.where(late, 0, 2))
+        pass_on(lines - 1)
+
+    @pl.when((line == 0) | (line == lines - 1))
+    def _():
+        for k in range(1, lines):
+            pass_on(line - k * toward)
 
     arrived(picked.at[pl.ds(0, n - 1)], turn_recv.at[0])
     group = lax.broadcasted_iota(jnp.int32, (rows, eig_count), 1) // rows
@@ -187,13 +264,13 @@
     sources = jnp.concatenate(chunks[0::2] + chunks[1::2], axis=0).astype(BF16)
     load_columns.wait()
     load_phases.wait()
-    arrived(sink.at[:, :, pl.ds(0, lines * rows), :], near_recv.at[0])
+    arrived(sink.at[pl.ds(0, lines)], near_recv.at[0])
 
     @pl.when(is_hub)
     def _():
         arrived(mfull.at[pl.ds(0, hubs - 1)], all_recv.at[0])
 
-    @pl.when(jnp.logical_not(is_hub))
+    @pl.when(is_leaf)
     def _():
         arrived(mfull, all_recv.at[0])
 
@@ -210,7 +287,13 @@
     )
     for pair in range(2):
         table = jnp.concatenate(
-            [sink[2 * pair + i].reshape(2 * eig_count, eig_count) for i in range(2)], axis=1
+            [
+                jnp.concatenate(
+                    [sink[owner, 4 * pair + 2 * i + c] for c in range(2) for owner in range(n)], axis=0
+                )
+                for i in range(2)
+            ],
+            axis=1,
         )
         result = jnp.dot(stacked, table, preferred_element_type=F32)
         for i in range(2):
@@ -237,13 +320,13 @@
 
     unit = 4 * rows
     plain = hubs * unit + 2 * lines * 8 * rows + (n - 1) * rows - 8 * rows
-    extra = (hubs - 1 + n - 1 - hubs) * unit
+    extra = (times * n - 2) * unit
 
     @pl.when(is_hub)
     def _():
         arrived(volume.at[pl.ds(0, plain + extra)], send_sem.at[0])
 
-    @pl.when(jnp.logical_not(is_hub))
+    @pl.when(is_leaf)
     def _():
         arrived(volume.at[pl.ds(0, plain)], send_sem.at[0])
 
@@ -257,6 +340,7 @@
 def on_device_kernel(eigvecs, perambulator, momenta, source_slots, gamma_columns, gamma_phases):
     sites, eig_count = eigvecs.shape[1], eigvecs.shape[4]
     n = lax.axis_size("space")
+    times = lax.axis_size("tm")
     rows = eig_count // n
     total_sites = sites * n
     gammas = gamma_columns.shape[0]
@@ -282,14 +366,17 @@
             pltpu.VMEM((sites * 6, eig_count), BF16),
             pltpu.VMEM((sites * 6, 2 * eig_count), BF16),
             pltpu.VMEM((stored, 4, 2, rows, eig_count), BF16),
-            pltpu.VMEM((4, 2, eig_count, eig_count), BF16),
+            pltpu.VMEM((n, 8, rows, eig_count), BF16),
             pltpu.VMEM((n, rows, 8 * rows), BF16),
             pltpu.VMEM((n, rows, 8 * rows), BF16),
             pltpu.VMEM((n // 2, 2 * rows, 2 * eig_count), WIRE),
-            pltpu.VMEM((n, 2 * rows, 2 * eig_count), WIRE),
+            pltpu.VMEM((times * n, 2 * rows, 2 * eig_count), WIRE),
+            pltpu.VMEM((times - 1, 2 * rows, 2 * eig_count), BF16),
             pltpu.VMEM((n // 2, 2 * rows, 2 * eig_count), BF16),
             pltpu.VMEM((2, 16, rows, eig_count), F32),
-            pltpu.VMEM((16 * eig_count, eig_count), BF16),
+            pltpu.VMEM((24 * eig_count, eig_count), BF16),
+            pltpu.SemaphoreType.REGULAR((1,)),
+            pltpu.SemaphoreType.REGULAR((n // 2,)),
             dma((6,)),
             dma((1,)),
             dma((1,)),
@@ -382,7 +469,7 @@
     n = lax.axis_size("space")
     rows = perambulator.shape[4]
     small = eigvecs.shape[1] % 16 == 0 and eigvecs.shape[4] == 128
-    if rows == 16 and n == 8 and momenta.shape[0] == 1 and small:
+    if rows == 16 and n == 8 and lax.axis_size("tm") == 2 and momenta.shape[0] == 1 and small:
         return on_device_kernel(eigvecs, perambulator, momenta, *rest)
     return on_device_plain(eigvecs, perambulator, momenta, *rest)
 

time: 15.8 us -> 14.5 us (0.918)
  Pallas kernels: 15.6 us -> 14.3 us
    pallas_call x1, Pallas kernels: 14.9 us -> 13.6 us  [on_device_kernel(): pl.pallas_call(body, out_shape=pltpu.VMEM((rows * gammas * 2, eig_count),...]
where the time goes in v3:
time: 14.5 us; the launch traced here: 14.3 us
  Pallas kernels  14.3 us (99%)
    pallas_call x1, Pallas kernels, on_device_kernel(): pl.pallas_call(body, out_shape=pltpu.VMEM((rows * gammas * 2, eig_count),...  13.6 us
    pallas_call x1, Pallas kernels, on_device_kernel(): pl.pallas_call(store_kernel, out_shape=jax.ShapeDtypeStruct(out.shape, F3...  0.69 us

profile of v3, /device:TPU:0, one launch (start us, length us, event | category | flops | bytes accessed | tf_op | source)
XLA Modules:
  0.0 14.3 jit_solution(14851287891475636453)
XLA Ops:
  0.0 13.6 %shard_map.64.source = f32[384,128]{1,0:T(8,128)S(1)} custom-call(s32[1,3]{1,0:T(1,128)} %momenta_hbm.1, s32[2]{0:T(128)} %slots_hbm.1, s32[4,12]{1,0:T(4,128)} %bitcast.9, s32[4,12]{1,0:T(4,128)} %bitcast.10, bf16[1728,128]{1,0:T(8,128)(2,1)} %bitcast.7, bf16[8,4,2,16,128]{4,3,2,1,0:T(8,128)(2,1)} %bitcast.8), custom_call_target="tpu_custom_call" | custom-call | tf_op jit(solution)/shard_map/pallas_call | solution.py:353
  13.6 0.7 %shard_map.65 = f32[384,128]{1,0:T(8,128)} custom-call(f32[384,128]{1,0:T(8,128)S(1)} %shard_map.64.source), custom_call_target="tpu_custom_call" | custom-call | tf_op jit(solution)/shard_map/pallas_call | solution.py:404

commit v4 on v3

--- a/solution.py
+++ b/solution.py
@@ -49,7 +49,7 @@
 def kernel(
     n, sites, extent_x, factor,
     momenta_hbm, slots_hbm, columns_hbm, phases_hbm, eig_hbm, per_hbm, out_ref,
-    momenta, slots, columns, phases, eig, eig32, waves, left, right, per, sink, turned, picked,
+    momenta, slots, columns, phases, picks, eig, eig32, waves, left, right, per, sink, turned, picked,
     part, sums, spread, mfull, blocks, volume,
     ready, reply, load_sem, send_sem, red_recv, all_recv, turn_recv, near_recv, line_recv,
 ):
@@ -88,22 +88,20 @@
             semaphore, inc=1, device_id={"space": peer, "tm": peer_time}, device_id_type=MESH
         )
 
-    def greets(source, source_time, target, target_time):
-        def hub(place, at):
-            return (place >= n // 4) & (place < n // 4 + hubs) & (at == hub_time)
-
-        step = target - source
-        ahead = (step > 0) & (lax.rem(step + n, 2) == 0)
-        pair = (lax.div(source, 2) == lax.div(target, 2)) & (step != 0)
-        near = (source_time == target_time) & (ahead | pair)
-        other = (step != 0) | (source_time != target_time)
-        return other & (hub(source, source_time) | hub(target, target_time) | near)
-
-    expected = 0
+    for j in range(hubs):
+        peer = j + n // 4
+        pl.when((me != peer) | is_leaf)(functools.partial(greet, barrier, peer, hub_time))
     for other in range(times):
-        for peer in range(n):
-            pl.when(greets(me, time, peer, other))(functools.partial(greet, barrier, peer, other))
-            expected = expected + greets(peer, other, me, time).astype(jnp.int32)
+        for peer in list(range(n // 4)) + list(reversed(range(n // 4, n))):
+            if n // 4 <= peer < n // 4 + hubs and other == times - 1:
+                continue
+            across = (line == peer // 2) & (side != peer % 2)
+            above = (side == peer % 2) & (line < peer // 2)
+            pl.when(is_hub | ((time == other) & (across | above)))(
+                functools.partial(greet, barrier, peer, other)
+            )
+    lower = jnp.where(time == hub_time, (line == lines - 1).astype(jnp.int32), line)
+    expected = jnp.where(is_hub, times * n - 1, hubs + 1 + lower)
 
     def remote(src, dst, recv, peer, peer_time=None):
         peer_time = time if peer_time is None else peer_time
@@ -132,7 +130,7 @@
                     greet(ready.at[0], me, other)
 
         for lower in range(lines - 1):
-            pl.when(lower < line)(
+            pl.when((lower < line) & ((lower != 1) | (line < lines - 1)))(
                 functools.partial(greet, reply.at[line], 2 * lower + side, time)
             )
 
@@ -159,7 +157,7 @@
     @pl.when(early)
     def _():
         enter()
-        send_sink(0)
+        send_sink(jnp.where(line == lines - 1, 0, 1))
         send_near()
 
     load_eig.wait()
@@ -169,22 +167,27 @@
         imag = eig32[pl.ds(2 * color + 1, sites, stride=6), :]
         wave_real = (waves[0] * real - waves[1] * imag).astype(BF16)
         wave_imag = (waves[1] * real + waves[0] * imag).astype(BF16)
-        low = pl.ds(2 * color * sites, sites)
-        high = pl.ds((2 * color + 1) * sites, sites)
-        left[low, :] = real.astype(BF16)
-        left[high, :] = imag.astype(BF16)
-        right[low, :eig_count] = wave_real
-        right[low, eig_count:] = wave_imag
-        right[high, :eig_count] = wave_imag
-        right[high, eig_count:] = -wave_real
+        span = pl.ds(color * sites, sites)
+        left[span, :eig_count] = real.astype(BF16)
+        left[span, eig_count:] = imag.astype(BF16)
+        right[span, :eig_count] = wave_real
+        right[span, eig_count:] = wave_imag
     whole = lax.dot_general(
         left[...], right[...], (((0,), (0,)), ((), ())), preferred_element_type=F32
     )
+    whole = jnp.concatenate(
+        [
+            whole[:eig_count, :eig_count] + whole[eig_count:, eig_count:],
+            whole[:eig_count, eig_count:] - whole[eig_count:, :eig_count],
+        ],
+        axis=1,
+    )
     part[...] = whole.astype(part.dtype).reshape(hubs, hub_rows, 2 * eig_count)
 
     def send_red():
         for i in range(hubs):
-            j = jnp.where(me < n // 2, hubs - 1 - i, i)
+            j = 2 * (i // 2) + (1 - i % 2) * (1 - 2 * side) + side
+            j = jnp.where(me < n // 2, (j + 2) % 4, j)
             copy = remote(
                 part.at[j], sums.at[time * n + me], red_recv.at[0], j + n // 4, hub_time
             )
@@ -201,7 +204,9 @@
     @pl.when(jnp.logical_not(early))
     def _():
         send_near()
-        pl.when(line > 0)(lambda: send_sink(0))
+        pl.when((line == 1) | (line == lines - 1))(lambda: send_sink(0))
+        pl.when(line == lines - 2)(lambda: send_sink(0))
+        pl.when(line == lines - 2)(lambda: send_sink(1))
 
     first = per[slots[0]].reshape(8 * rows, eig_count).astype(F32)
     turned[...] = first.T.astype(BF16).reshape(n, rows, 8 * rows)
@@ -214,8 +219,8 @@
 
     pl.when(is_leaf)(lambda: pl.semaphore_wait(ready.at[0], 1))
     send_turned()
-    pl.when(line < lines - 1)(lambda: send_up(lines - 1))
-    pl.when(late)(lambda: send_sink(1))
+    pl.when((line == 0) | (line == lines - 2))(lambda: send_up(lines - 1))
+    pl.when(line == lines - 1)(lambda: send_sink(1))
     pl.when(line == lines - 1)(lambda: send_sink(2))
 
     def forward(origin):
@@ -226,6 +231,8 @@
     def pass_on(origin):
         owner = forward(origin)
         remote(sink.at[owner], sink.at[owner], near_recv.at[0], partner).start()
+
+    inner_line = (line > 0) & (line < lines - 1)
 
     @pl.when(is_hub)
     def _():
@@ -241,16 +248,34 @@
                 peer = k + (k >= me).astype(jnp.int32) if own else k
                 remote(source, mfull.at[here], all_recv.at[0], peer, other).start()
 
-    @pl.when((line > 0) & (line < lines - 1))
-    def _():
-        pass_on(jnp.where(late, 1, 0))
-        pass_on(jnp.where(late, 0, 2))
-        pass_on(lines - 1)
-
-    @pl.when((line == 0) | (line == lines - 1))
-    def _():
-        for k in range(1, lines):
-            pass_on(line - k * toward)
+    relays = inner_line & (late | (time == 0))
+
+    @pl.when(inner_line & jnp.logical_not(relays))
+    def _():
+        pass_on(line - toward)
+
+    @pl.when(relays)
+    def _():
+        origin = line - toward
+        owner = forward(origin)
+        ends = me + 2 * toward
+        block = sink.at[owner]
+        remote(block, block, line_recv.at[line + toward], ends + 1 - 2 * side).start()
+        remote(block, block, line_recv.at[origin], ends).start()
+        remote(block, block, near_recv.at[0], partner).start()
+
+    @pl.when(inner_line)
+    def _():
+        pass_on(line + toward)
+        pass_on(line - 2 * toward)
+
+    plain_end = (line == 0) & (time == hub_time)
+
+    @pl.when(jnp.logical_not(inner_line))
+    def _():
+        pass_on(line - toward)
+        pl.when(plain_end)(lambda: pass_on(line - 2 * toward))
+        pass_on(line - 3 * toward)
 
     arrived(picked.at[pl.ds(0, n - 1)], turn_recv.at[0])
     group = lax.broadcasted_iota(jnp.int32, (rows, eig_count), 1) // rows
@@ -264,7 +289,22 @@
     sources = jnp.concatenate(chunks[0::2] + chunks[1::2], axis=0).astype(BF16)
     load_columns.wait()
     load_phases.wait()
-    arrived(sink.at[pl.ds(0, lines)], near_recv.at[0])
+    for g in range(gammas):
+        for spin in range(4):
+            phase = phases[spin, g]
+            place = spin * 4 + columns[spin, g]
+            picks[0, 4 * g + spin] = phase * 16 + place
+            picks[1, 4 * g + spin] = lax.rem(phase + 3, 4) * 16 + place
+
+    @pl.when(inner_line | plain_end)
+    def _():
+        arrived(sink.at[pl.ds(0, lines)], near_recv.at[0])
+
+    @pl.when(jnp.logical_not(inner_line | plain_end))
+    def _():
+        forward(line - 2 * toward)
+        arrived(sink.at[me], line_recv.at[line])
+        arrived(sink.at[pl.ds(0, lines - 1)], near_recv.at[0])
 
     @pl.when(is_hub)
     def _():
@@ -297,38 +337,40 @@
         )
         result = jnp.dot(stacked, table, preferred_element_type=F32)
         for i in range(2):
-            for part_of in range(2):
-                for spin in range(4):
-                    base = (part_of * 4 + spin) * rows
-                    blocks[part_of, spin * 4 + 2 * pair + i] = result[
-                        base : base + rows, i * eig_count : (i + 1) * eig_count
-                    ]
+            for spin in range(4):
+                place = spin * 4 + 2 * pair + i
+                columns_of = slice(i * eig_count, (i + 1) * eig_count)
+                real = result[spin * rows : (spin + 1) * rows, columns_of]
+                imag = result[(4 + spin) * rows : (5 + spin) * rows, columns_of]
+                for turn, block in enumerate((real, -imag, -real, imag)):
+                    blocks[turn * 16 + place] = block
     for g in range(gammas):
-        real = imag = None
-        for spin in range(4):
-            phase = phases[spin, g]
-            odd = phase % 2
-            index = spin * 4 + columns[spin, g]
-            sign_real = jnp.where((phase == 0) | (phase == 3), 1.0, -1.0).astype(F32)
-            sign_imag = jnp.where(phase < 2, 1.0, -1.0).astype(F32)
-            term_real = sign_real * blocks[odd, index]
-            term_imag = sign_imag * blocks[1 - odd, index]
-            real = term_real if real is None else real + term_real
-            imag = term_imag if imag is None else imag + term_imag
-        out_ref[pl.ds(2 * g, rows, stride=2 * gammas), :] = real
-        out_ref[pl.ds(2 * g + 1, rows, stride=2 * gammas), :] = imag
+        for which in range(2):
+            term = blocks[picks[which, 4 * g]]
+            for spin in range(1, 4):
+                term = term + blocks[picks[which, 4 * g + spin]]
+            out_ref[pl.ds(2 * g + which, rows, stride=2 * gammas), :] = term
 
     unit = 4 * rows
     plain = hubs * unit + 2 * lines * 8 * rows + (n - 1) * rows - 8 * rows
     extra = (times * n - 2) * unit
 
-    @pl.when(is_hub)
-    def _():
-        arrived(volume.at[pl.ds(0, plain + extra)], send_sem.at[0])
-
-    @pl.when(is_leaf)
-    def _():
-        arrived(volume.at[pl.ds(0, plain)], send_sem.at[0])
+    block = 8 * rows
+    direct = time == hub_time
+    changes = (
+        (inner_line & (late | jnp.logical_not(direct)) & jnp.logical_not(late & direct), block),
+        (late & inner_line & direct, 2 * block),
+        (jnp.logical_not(late) & inner_line & direct, -block),
+        (plain_end, 0),
+        (jnp.logical_not(inner_line | plain_end), -block),
+    )
+    for hub, spreading in ((is_hub, extra), (is_leaf, 0)):
+        for some, change in changes:
+            pl.when(hub & some)(
+                functools.partial(
+                    arrived, volume.at[pl.ds(0, plain + spreading + change)], send_sem.at[0]
+                )
+            )
 
 
 def store_kernel(source, target, sem):
@@ -360,11 +402,12 @@
             pltpu.SMEM(source_slots.shape, jnp.int32),
             pltpu.SMEM((4, gammas), jnp.int32),
             pltpu.SMEM((4, gammas), jnp.int32),
+            pltpu.SMEM((2, 4 * gammas), jnp.int32),
             pltpu.VMEM((sites * 6, eig_count), BF16),
             pltpu.VMEM((sites * 6, eig_count), F32),
             pltpu.VMEM((2, sites, eig_count), F32),
-            pltpu.VMEM((sites * 6, eig_count), BF16),
-            pltpu.VMEM((sites * 6, 2 * eig_count), BF16),
+            pltpu.VMEM((sites * 3, 2 * eig_count), BF16),
+            pltpu.VMEM((sites * 3, 2 * eig_count), BF16),
             pltpu.VMEM((stored, 4, 2, rows, eig_count), BF16),
             pltpu.VMEM((n, 8, rows, eig_count), BF16),
             pltpu.VMEM((n, rows, 8 * rows), BF16),
@@ -373,7 +416,7 @@
             pltpu.VMEM((times * n, 2 * rows, 2 * eig_count), WIRE),
             pltpu.VMEM((times - 1, 2 * rows, 2 * eig_count), BF16),
             pltpu.VMEM((n // 2, 2 * rows, 2 * eig_count), BF16),
-            pltpu.VMEM((2, 16, rows, eig_count), F32),
+            pltpu.VMEM((64, rows, eig_count), F32),
             pltpu.VMEM((24 * eig_count, eig_count), BF16),
             pltpu.SemaphoreType.REGULAR((1,)),
             pltpu.SemaphoreType.REGULAR((n // 2,)),

time: 14.5 us -> 14 us (0.966)
  Pallas kernels: 14.3 us -> 13.8 us
    pallas_call x1, Pallas kernels: 13.6 us -> 13.1 us  [on_device_kernel(): pl.pallas_call(body, out_shape=pltpu.VMEM((rows * gammas * 2, eig_count),...]
where the time goes in v4:
time: 14 us; the launch traced here: 13.8 us
  Pallas kernels  13.8 us (99%)
    pallas_call x1, Pallas kernels, on_device_kernel(): pl.pallas_call(body, out_shape=pltpu.VMEM((rows * gammas * 2, eig_count),...  13.1 us
    pallas_call x1, Pallas kernels, on_device_kernel(): pl.pallas_call(store_kernel, out_shape=jax.ShapeDtypeStruct(out.shape, F3...  0.69 us

profile of v4, /device:TPU:0, one launch (start us, length us, event | category | flops | bytes accessed | tf_op | source)
XLA Modules:
  0.0 13.8 jit_solution(7136204095775059599)
XLA Ops:
  0.0 13.1 %shard_map.64.source = f32[384,128]{1,0:T(8,128)S(1)} custom-call(s32[1,3]{1,0:T(1,128)} %momenta_hbm.1, s32[2]{0:T(128)} %slots_hbm.1, s32[4,12]{1,0:T(4,128)} %bitcast.9, s32[4,12]{1,0:T(4,128)} %bitcast.10, bf16[1728,128]{1,0:T(8,128)(2,1)} %bitcast.7, bf16[8,4,2,16,128]{4,3,2,1,0:T(8,128)(2,1)} %bitcast.8), custom_call_target="tpu_custom_call" | custom-call | tf_op jit(solution)/shard_map/pallas_call | solution.py:395
  13.1 0.7 %shard_map.65 = f32[384,128]{1,0:T(8,128)} custom-call(f32[384,128]{1,0:T(8,128)S(1)} %shard_map.64.source), custom_call_target="tpu_custom_call" | custom-call | tf_op jit(solution)/shard_map/pallas_call | solution.py:447

commit v5 on v4

--- a/solution.py
+++ b/solution.py
@@ -76,9 +76,9 @@
     load_eig = pltpu.make_async_copy(eig_hbm, eig, load_sem.at[1])
     load_slots = pltpu.make_async_copy(slots_hbm, slots, load_sem.at[2])
     load_momenta = pltpu.make_async_copy(momenta_hbm, momenta, load_sem.at[3])
-    load_columns = pltpu.make_async_copy(columns_hbm, columns, load_sem.at[4])
-    load_phases = pltpu.make_async_copy(phases_hbm, phases, load_sem.at[5])
-    for load in (load_slots, load_momenta, load_per, load_eig, load_columns, load_phases):
+    load_columns = pltpu.make_async_copy(columns_hbm, columns, load_sem.at[2])
+    load_phases = pltpu.make_async_copy(phases_hbm, phases, load_sem.at[3])
+    for load in (load_slots, load_momenta, load_per, load_eig):
         load.start()
 
     barrier = pltpu.get_barrier_semaphore()
@@ -131,11 +131,11 @@
 
         for lower in range(lines - 1):
             pl.when((lower < line) & ((lower != 1) | (line < lines - 1)))(
-                functools.partial(greet, reply.at[line], 2 * lower + side, time)
+                functools.partial(greet, reply.at[jnp.maximum(line, 1) - 1], 2 * lower + side, time)
             )
 
     def send_up(target):
-        pl.semaphore_wait(reply.at[target], 1)
+        pl.semaphore_wait(reply.at[target - 1], 1)
         send_sink(target)
 
     def send_sink(target):
@@ -189,7 +189,7 @@
             j = 2 * (i // 2) + (1 - i % 2) * (1 - 2 * side) + side
             j = jnp.where(me < n // 2, (j + 2) % 4, j)
             copy = remote(
-                part.at[j], sums.at[time * n + me], red_recv.at[0], j + n // 4, hub_time
+                part.at[j], sums.at[time * n + me], red_recv.at[time], j + n // 4, hub_time
             )
             pl.when((slot != j) | is_leaf)(copy.start)
 
@@ -208,6 +208,8 @@
         pl.when(line == lines - 2)(lambda: send_sink(0))
         pl.when(line == lines - 2)(lambda: send_sink(1))
 
+    load_columns.start()
+    load_phases.start()
     first = per[slots[0]].reshape(8 * rows, eig_count).astype(F32)
     turned[...] = first.T.astype(BF16).reshape(n, rows, 8 * rows)
     picked[me] = turned[me]
@@ -236,12 +238,15 @@
 
     @pl.when(is_hub)
     def _():
-        arrived(sums.at[pl.ds(0, times * n - 1)], red_recv.at[0])
+        sums[time * n + me] = part[here]
         for other in range(times):
             own = other == times - 1
-            total = part[here].astype(F32) if own else sums[other * n + me].astype(F32)
+            if own:
+                pl.when(line == 1)(lambda: pass_on(0))
+            arrived(sums.at[pl.ds(0, n - own)], red_recv.at[other])
+            total = sums[other * n].astype(F32)
             for k in range(1, n):
-                total = total + sums[other * n + lax.rem(me + k, n)].astype(F32)
+                total = total + sums[other * n + k].astype(F32)
             source = mfull.at[here] if own else spread.at[other]
             source[...] = total.astype(BF16)
             for k in range(n - own):
@@ -266,7 +271,7 @@
 
     @pl.when(inner_line)
     def _():
-        pass_on(line + toward)
+        pl.when(late | (time < hub_time))(lambda: pass_on(line + toward))
         pass_on(line - 2 * toward)
 
     plain_end = (line == 0) & (time == hub_time)
@@ -419,10 +424,10 @@
             pltpu.VMEM((64, rows, eig_count), F32),
             pltpu.VMEM((24 * eig_count, eig_count), BF16),
             pltpu.SemaphoreType.REGULAR((1,)),
-            pltpu.SemaphoreType.REGULAR((n // 2,)),
-            dma((6,)),
+            pltpu.SemaphoreType.REGULAR((n // 2 - 1,)),
+            dma((4,)),
             dma((1,)),
-            dma((1,)),
+            dma((2,)),
             dma((1,)),
             dma((1,)),
             dma((1,)),

time: 14 us -> 13.9 us (level)
  no operation moved by 1% of the time
where the time goes in v5:
time: 13.9 us; the launch traced here: 13.8 us
  Pallas kernels  13.8 us (99%)
    pallas_call x1, Pallas kernels, on_device_kernel(): pl.pallas_call(body, out_shape=pltpu.VMEM((rows * gammas * 2, eig_count),...  13.1 us
    pallas_call x1, Pallas kernels, on_device_kernel(): pl.pallas_call(store_kernel, out_shape=jax.ShapeDtypeStruct(out.shape, F3...  0.69 us

profile of v5, /device:TPU:0, one launch (start us, length us, event | category | flops | bytes accessed | tf_op | source)
XLA Modules:
  0.0 13.8 jit_solution(3581806578135187168)
XLA Ops:
  0.0 13.1 %shard_map.64.source = f32[384,128]{1,0:T(8,128)S(1)} custom-call(s32[1,3]{1,0:T(1,128)} %momenta_hbm.1, s32[2]{0:T(128)} %slots_hbm.1, s32[4,12]{1,0:T(4,128)} %bitcast.9, s32[4,12]{1,0:T(4,128)} %bitcast.10, bf16[1728,128]{1,0:T(8,128)(2,1)} %bitcast.7, bf16[8,4,2,16,128]{4,3,2,1,0:T(8,128)(2,1)} %bitcast.8), custom_call_target="tpu_custom_call" | custom-call | tf_op jit(solution)/shard_map/pallas_call | solution.py:400
  13.1 0.7 %shard_map.65 = f32[384,128]{1,0:T(8,128)} custom-call(f32[384,128]{1,0:T(8,128)S(1)} %shard_map.64.source), custom_call_target="tpu_custom_call" | custom-call | tf_op jit(solution)/shard_map/pallas_call | solution.py:452

commit v6 on v5

--- a/solution.py
+++ b/solution.py
@@ -17,12 +17,17 @@
 VMEM_LIMIT = 32 * 1024 * 1024
 
 
-def site_phases(momenta_at, first_site, site_count, extent_x, shape):
+def site_coords(first_site, shape):
     site = (lax.broadcasted_iota(jnp.int32, shape, 0) + first_site).astype(F32)
     lines = jnp.floor((site + 0.5) * (1.0 / LZ))
     coord_x = jnp.floor((lines + 0.5) * (1.0 / LY))
     coord_y = lines - LY * coord_x
     coord_z = site - LZ * lines
+    return coord_x, coord_y, coord_z
+
+
+def site_phases(momenta_at, coords, extent_x, shape):
+    coord_x, coord_y, coord_z = coords
 
     def share(momentum, coord, extent):
         turn = momentum.astype(F32) * coord * (1.0 / extent)
@@ -49,7 +54,7 @@
 def kernel(
     n, sites, extent_x, factor,
     momenta_hbm, slots_hbm, columns_hbm, phases_hbm, eig_hbm, per_hbm, out_ref,
-    momenta, slots, columns, phases, picks, eig, eig32, waves, left, right, per, sink, turned, picked,
+    momenta, slots, columns, phases, picks, eig, eig32, coords, waves, left, right, per, sink, turned, picked,
     part, sums, spread, mfull, blocks, volume,
     ready, reply, load_sem, send_sem, red_recv, all_recv, turn_recv, near_recv, line_recv,
 ):
@@ -144,8 +149,12 @@
     def send_near():
         remote(sink_of(me), sink_of(me), near_recv.at[0], partner).start()
 
+    for i, coord in enumerate(site_coords(me * sites, (sites, eig_count))):
+        coords[i] = coord
     load_momenta.wait()
-    cosine, sine = site_phases(lambda i: momenta[0, i], me * sites, sites, extent_x, (sites, eig_count))
+    cosine, sine = site_phases(
+        lambda i: momenta[0, i], [coords[i] for i in range(3)], extent_x, (sites, eig_count)
+    )
     waves[0] = cosine
     waves[1] = sine
     load_slots.wait()
@@ -410,6 +419,7 @@
             pltpu.SMEM((2, 4 * gammas), jnp.int32),
             pltpu.VMEM((sites * 6, eig_count), BF16),
             pltpu.VMEM((sites * 6, eig_count), F32),
+            pltpu.VMEM((3, sites, eig_count), F32),
             pltpu.VMEM((2, sites, eig_count), F32),
             pltpu.VMEM((sites * 3, 2 * eig_count), BF16),
             pltpu.VMEM((sites * 3, 2 * eig_count), BF16),
@@ -476,7 +486,7 @@
     tables = []
     for p in range(momenta.shape[0]):
         cosine, sine = site_phases(
-            lambda i, p=p: momenta[p, i], first_site, sites, extent_x, (sites, 1, 1)
+            lambda i, p=p: momenta[p, i], site_coords(first_site, (sites, 1, 1)), extent_x, (sites, 1, 1)
         )
         wave_real = cosine * real - sine * imag
         wave_imag = sine * real + cosine * imag

time: 13.9 us -> 13.9 us (level)
  no operation moved by 1% of the time
where the time goes in v6:
time: 13.9 us; the launch traced here: 13.8 us
  Pallas kernels  13.8 us (99%)
    pallas_call x1, Pallas kernels, on_device_kernel(): pl.pallas_call(body, out_shape=pltpu.VMEM((rows * gammas * 2, eig_count),...  13.1 us
    pallas_call x1, Pallas kernels, on_device_kernel(): pl.pallas_call(store_kernel, out_shape=jax.ShapeDtypeStruct(out.shape, F3...  0.69 us

profile of v6, /device:TPU:0, one launch (start us, length us, event | category | flops | bytes accessed | tf_op | source)
XLA Modules:
  0.0 13.8 jit_solution(2525153660622626536)
XLA Ops:
  0.0 13.1 %shard_map.64.source = f32[384,128]{1,0:T(8,128)S(1)} custom-call(s32[1,3]{1,0:T(1,128)} %momenta_hbm.1, s32[2]{0:T(128)} %slots_hbm.1, s32[4,12]{1,0:T(4,128)} %bitcast.9, s32[4,12]{1,0:T(4,128)} %bitcast.10, bf16[1728,128]{1,0:T(8,128)(2,1)} %bitcast.7, bf16[8,4,2,16,128]{4,3,2,1,0:T(8,128)(2,1)} %bitcast.8), custom_call_target="tpu_custom_call" | custom-call | tf_op jit(solution)/shard_map/pallas_call | solution.py:409
  13.1 0.7 %shard_map.65 = f32[384,128]{1,0:T(8,128)} custom-call(f32[384,128]{1,0:T(8,128)S(1)} %shard_map.64.source), custom_call_target="tpu_custom_call" | custom-call | tf_op jit(solution)/shard_map/pallas_call | solution.py:462

commit v7 on v6

--- a/solution.py
+++ b/solution.py
@@ -213,7 +213,7 @@
     @pl.when(jnp.logical_not(early))
     def _():
         send_near()
-        pl.when((line == 1) | (line == lines - 1))(lambda: send_sink(0))
+        pl.when(line == 1)(lambda: send_sink(0))
         pl.when(line == lines - 2)(lambda: send_sink(0))
         pl.when(line == lines - 2)(lambda: send_sink(1))
 
@@ -231,6 +231,7 @@
     pl.when(is_leaf)(lambda: pl.semaphore_wait(ready.at[0], 1))
     send_turned()
     pl.when((line == 0) | (line == lines - 2))(lambda: send_up(lines - 1))
+    pl.when((line == lines - 1) & (time == hub_time))(lambda: send_sink(0))
     pl.when(line == lines - 1)(lambda: send_sink(1))
     pl.when(line == lines - 1)(lambda: send_sink(2))
 

time: 13.9 us -> 13.9 us (level)
  no operation moved by 1% of the time
where the time goes in v7:
time: 13.9 us; the launch traced here: 13.7 us
  Pallas kernels  13.7 us (99%)
    pallas_call x1, Pallas kernels, on_device_kernel(): pl.pallas_call(body, out_shape=pltpu.VMEM((rows * gammas * 2, eig_count),...  13 us
    pallas_call x1, Pallas kernels, on_device_kernel(): pl.pallas_call(store_kernel, out_shape=jax.ShapeDtypeStruct(out.shape, F3...  0.69 us

profile of v7, /device:TPU:0, one launch (start us, length us, event | category | flops | bytes accessed | tf_op | source)
XLA Modules:
  0.0 13.7 jit_solution(7581789042188951401)
XLA Ops:
  0.0 13.0 %shard_map.64.source = f32[384,128]{1,0:T(8,128)S(1)} custom-call(s32[1,3]{1,0:T(1,128)} %momenta_hbm.1, s32[2]{0:T(128)} %slots_hbm.1, s32[4,12]{1,0:T(4,128)} %bitcast.9, s32[4,12]{1,0:T(4,128)} %bitcast.10, bf16[1728,128]{1,0:T(8,128)(2,1)} %bitcast.7, bf16[8,4,2,16,128]{4,3,2,1,0:T(8,128)(2,1)} %bitcast.8), custom_call_target="tpu_custom_call" | custom-call | tf_op jit(solution)/shard_map/pallas_call | solution.py:410
  13.0 0.7 %shard_map.65 = f32[384,128]{1,0:T(8,128)} custom-call(f32[384,128]{1,0:T(8,128)S(1)} %shard_map.64.source), custom_call_target="tpu_custom_call" | custom-call | tf_op jit(solution)/shard_map/pallas_call | solution.py:463
